TPU v7x, 32 devices: a whole 2x2x4 slice. The times are simulated.
32 devices in a mesh: rows: 4 (over y, core), cols: 8 (over z, x).
Axes of the slice: x: 2, y: 2, z: 4, core: 2. Of those that a mesh axis runs over, the one named last changes fastest.
Arguments:
- single: bfloat16 [512, 1024], P('rows'), may hold values from -6 to 6
- pair: bfloat16 [512, 512, 128], P('rows', 'cols'), may hold values from -6 to 6
- residue_mask: int32 [512], replicated, may hold values from 0 to 1, as said below
- w_bias: bfloat16 [128, 32], replicated, may hold values from -40 to 40
- w_project: bfloat16 [4, 1024, 1024], P(None, None, 'cols'), may hold values from -0.1875 to 0.1875
- w_out: bfloat16 [1024, 1024], replicated, may hold values from -0.1875 to 0.1875
- w_factors: bfloat16 [1024, 128], replicated, may hold values from -0.1875 to 0.1875
- w_pairout: bfloat16 [128, 128], replicated, may hold values from -0.5 to 0.5
- w_up: bfloat16 [128, 512], replicated, may hold values from -0.5 to 0.5
- w_down: bfloat16 [512, 128], replicated, may hold values from -0.25 to 0.25
Outputs:
- single_out: bfloat16 [512, 1024], P('rows')
- pair_out: bfloat16 [512, 512, 128], P('rows', 'cols')
Inputs may be any that keep to these rules, and one draw needn't show every extreme that they name: residue_mask is 1 on a leading run of at least 256 positions and 0 after it.
All inputs are finite; a program needn't handle non-finite values.
Results may differ from a plain program's by a relative error of at most 0.01.
The roundings to bfloat16 on the way count: a program that leaves them out, or rounds other values in their place, can miss the bound.
Values may be sent and summed in bfloat16 or wider, within the bound.
A program may use at most 64 MiB of HBM per device.

v0:
```python
import math
import jax
import jax.numpy as jnp
from jax import lax
from jax.sharding import PartitionSpec as P

epsilon = 1e-05


def from_root(value, axis, root):
    mine = lax.axis_index(axis) == root
    return lax.psum(jnp.where(mine, value, jnp.zeros_like(value)), axis)


def layer_norm(values):
    values = values.astype(jnp.float32)
    centred = values - jnp.mean(values, -1, keepdims=True)
    return centred * lax.rsqrt(jnp.mean(centred * centred, -1, keepdims=True) + epsilon)


def per_device(
    single, pair, residue_mask, w_bias, w_project, w_out, w_factors, w_pairout, w_up, w_down
):
    tile_rows = pair.shape[0]
    tile_cols = pair.shape[1]
    normed_pair = layer_norm(pair).astype(jnp.bfloat16)
    bias_local = jnp.einsum(
        "rcp,ph->hrc", normed_pair, w_bias, preferred_element_type=jnp.float32
    ).astype(jnp.bfloat16)
    normed_single = layer_norm(single).astype(jnp.bfloat16)
    projected = jnp.einsum(
        "rs,fsc->frc", normed_single, w_project, preferred_element_type=jnp.float32
    )
    query_rows = projected[0].astype(jnp.bfloat16)
    key_local = projected[1].astype(jnp.bfloat16)
    value_local = projected[2].astype(jnp.bfloat16)
    gate_values = jax.nn.sigmoid(projected[3])
    first_residue = lax.axis_index("cols") * tile_cols
    owner_row = first_residue // tile_rows
    offset_rows = first_residue - owner_row * tile_rows
    bias_heads = lax.all_to_all(bias_local, "cols", split_axis=0, concat_axis=2, tiled=True)
    key_rows, value_rows = (
        lax.all_gather(key_local, "rows", axis=0, tiled=True),
        lax.all_gather(value_local, "rows", axis=0, tiled=True),
    )
    heads_here = bias_heads.shape[0]
    head_width = query_rows.shape[1] // heads_here
    residues = key_rows.shape[0]
    query_split = query_rows.reshape(tile_rows, heads_here, head_width)
    key_split = key_rows.reshape(residues, heads_here, head_width)
    value_split = value_rows.reshape(residues, heads_here, head_width)
    score_scale = 1.0 / math.sqrt(head_width)
    scores = jnp.einsum(
        "rhd,lhd->hrl", query_split, key_split, preferred_element_type=jnp.float32
    ) * score_scale + bias_heads.astype(jnp.float32)
    key_valid = (residue_mask > 0)[None, None, :]
    scores = jnp.where(key_valid, scores, -jnp.inf)
    weights = jax.nn.softmax(scores, axis=-1).astype(jnp.bfloat16)
    attended = jnp.einsum("hrl,lhd->rhd", weights, value_split, preferred_element_type=jnp.float32)
    attended = attended.reshape(tile_rows, heads_here * head_width)
    mixed = (attended * gate_values).astype(jnp.bfloat16)
    whole_heads = lax.all_gather(mixed, "cols", axis=1, tiled=True)
    head_total = jnp.dot(whole_heads, w_out, preferred_element_type=jnp.float32)
    single_out = (single.astype(jnp.float32) + head_total).astype(jnp.bfloat16)
    normed_out = layer_norm(single_out).astype(jnp.bfloat16)
    factors = jnp.dot(normed_out, w_factors, preferred_element_type=jnp.float32).astype(
        jnp.bfloat16
    )
    factor_width = factors.shape[1] // 2
    left_factor = factors[:, :factor_width]
    right_local = factors[:, factor_width:]
    right_piece = lax.dynamic_slice_in_dim(right_local, offset_rows, tile_cols, 0)
    right_cols = from_root(right_piece, "rows", owner_row)
    block_rows = math.gcd(tile_rows, max(1, 4096 // tile_cols))
    count_blocks = tile_rows // block_rows

    def update_block(operands):
        pair_block, left_block = operands
        left_wide = left_block.astype(jnp.float32)[:, None, :]
        right_wide = right_cols.astype(jnp.float32)[None, :, :]
        paired = jnp.concatenate([left_wide * right_wide, left_wide - right_wide], -1).astype(
            jnp.bfloat16
        )
        pair_mid = (
            pair_block.astype(jnp.float32)
            + jnp.einsum("rcq,qp->rcp", paired, w_pairout, preferred_element_type=jnp.float32)
        ).astype(jnp.bfloat16)
        normed_mid = layer_norm(pair_mid).astype(jnp.bfloat16)
        hidden = jax.nn.relu(
            jnp.einsum("rcp,pk->rck", normed_mid, w_up, preferred_element_type=jnp.float32)
        ).astype(jnp.bfloat16)
        return (
            pair_mid.astype(jnp.float32)
            + jnp.einsum("rck,kp->rcp", hidden, w_down, preferred_element_type=jnp.float32)
        ).astype(jnp.bfloat16)

    updated = lax.map(
        update_block,
        (
            pair.reshape(count_blocks, block_rows, tile_cols, pair.shape[2]),
            left_factor.reshape(count_blocks, block_rows, factor_width),
        ),
    )
    return (single_out, updated.reshape(pair.shape))


def solution(mesh):
    return jax.shard_map(
        per_device,
        mesh=mesh,
        in_specs=(
            P("rows", None),
            P("rows", "cols", None),
            P(),
            P(),
            P(None, None, "cols"),
            P(),
            P(),
            P(),
            P(),
            P(),
        ),
        out_specs=(P("rows", None), P("rows", "cols", None)),
        check_vma=False,
    )
```

profile of v0, /device:TPU:0, one launch (start us, length us, event | category | flops | bytes accessed | tf_op | source)
XLA Modules:
  0.0 100.3 jit_solution(4183967973226425376)
XLA Ops:
  0.7 2.9 %convert_reduce_fusion.1 = f32[128,64]{1,0:T(8,128)S(1)} fusion(bf16[128,64,128]{2,1,0:T(8,128)(2,1)} %param.13), kind=kLoop, calls=%fused_computation.33 | loop fusion | flops 2088960 | bytes 2129920 | tf_op jit(solution)/shard_map/reduce_sum | solution.py:17
  3.6 2.7 %fusion.30 = f32[128,64]{1,0:T(8,128)S(1)} fusion(bf16[128,64,128]{2,1,0:T(8,128)(2,1)S(1)} %copy-done.1, f32[128,64]{1,0:T(8,128)S(1)} %broadcast_multiply_fusion.1), kind=kLoop, calls=%fused_computation.36 | loop fusion | flops 4186112 | bytes 2162688 | tf_op jit(solution)/shard_map/reduce_sum | solution.py:18
  6.4 3.4 %fusion.31 = bf16[128,64,128]{2,1,0:T(8,128)(2,1)S(1)} fusion(bf16[128,64,128]{2,1,0:T(8,128)(2,1)S(1)} %copy-done.1, f32[128,64]{1,0:T(8,128)S(1)} %add_rsqrt_fusion.1, f32[128,64]{1,0:T(8,128)S(1)} %broadcast_multiply_fusion.1), kind=kLoop, calls=%fused_computation.37 | loop fusion | flops 4194304 | bytes 4259840 | tf_op jit(solution)/shard_map/convert_element_type | solution.py:26
  9.8 1.4 %fusion.41 = bf16[32,128,64]{1,0,2:T(8,128)(2,1)S(1)} fusion(bf16[128,64,128]{2,1,0:T(8,128)(2,1)S(1)} %fusion.31, bf16[128,32]{0,1:T(8,128)(2,1)S(1)} %copy-done.7), kind=kOutput, calls=%fused_computation.46 | convolution fusion | flops 67371008 | bytes 2629632 | tf_op jit(solution)/shard_map/rcp,ph->hrc/dot_general | solution.py:27
  11.1 1.0 %copy.31 = bf16[32,128,64]{1,2,0:T(8,128)(2,1)} copy(bf16[32,128,64]{1,0,2:T(8,128)(2,1)S(1)} %fusion.41) | data formatting | bytes 1048576 | tf_op jit(solution)/shard_map/convert_element_type | solution.py:29
  12.2 7.3 %all-to-all-start = ((bf16[32,128,64]{1,2,0:T(8,128)(2,1)}), bf16[32,128,64]{1,2,0:T(8,128)(2,1)}, u32[]{:S(2)}, u32[]{:S(2)}) async-start(bf16[32,128,64]{1,2,0:T(8,128)(2,1)} %copy.31), calls=%async_computation | async-start | bytes 1048576 | tf_op jit(solution)/shard_map/all_to_all | solution.py:41
  19.9 1.5 %copy.29 = bf16[4,1024,128]{1,2,0:T(8,128)(2,1)S(1)} copy(bf16[4,1024,128]{2,1,0:T(8,128)(2,1)} %param.16) | data formatting | bytes 2097152 | tf_op args[4]
  23.2 5.4 %all-gather.1 = bf16[1,512,128]{1,2,0:T(8,128)(2,1)S(1)} all-gather(bf16[1,128,128]{1,2,0:T(8,128)(2,1)S(1)} %get-tuple-element.97), channel_id=3, replica_groups=mesh['rows'=4,'cols'=8] {'rows'}, dimensions={1}, use_global_device_ids=true | all-gather | bytes 163840 | tf_op jit(solution)/shard_map/all_gather | solution.py:43
  28.7 5.9 %all-gather = bf16[1,512,128]{1,2,0:T(8,128)(2,1)} all-gather(bf16[1,128,128]{1,2,0:T(8,128)(2,1)S(1)} %get-tuple-element.99), channel_id=2, replica_groups=mesh['rows'=4,'cols'=8] {'rows'}, dimensions={1}, use_global_device_ids=true | all-gather | bytes 163840 | tf_op jit(solution)/shard_map/all_gather | solution.py:44
  34.5 1.1 %convert_bitcast_fusion = f32[4,128,8,64]{1,3,0,2:T(8,128)S(1)} fusion(bf16[8,4,128,64]{2,3,1,0:T(8,128)(2,1)} %bitcast.28), kind=kLoop, calls=%fused_computation.50 | loop fusion | flops 262144 | bytes 1572864 | tf_op jit(solution)/shard_map/convert_element_type | solution.py:55
  35.8 1.3 %copy.33 = f32[4,128,512]{2,1,0:T(8,128)} copy(f32[4,128,512]{1,2,0:T(8,128)S(1)} %bitcast.77) | data formatting | bytes 2097152 | tf_op jit(solution)/shard_map/convert_element_type | solution.py:55
  37.1 1.6 %fusion.37 = f32[4,128,512]{2,1,0:T(8,128)S(1)} fusion(f32[4,128,512]{2,1,0:T(8,128)} %copy.33, bf16[128,4,32]{0,2,1:T(8,128)(2,1)} %bitcast.82, bf16[512,4,32]{0,2,1:T(8,128)(2,1)S(1)} %bitcast.80, pred[512]{0:T(512)(128)(4,1)S(1)} %broadcast_compare_fusion), kind=kOutput, calls=%fused_computation.44 | convolution fusion | flops 17563648 | bytes 2261504 | tf_op jit(solution)/shard_map/rhd,lhd->hrl/dot_general | solution.py:53
  39.0 1.9 %fusion.53 = f32[4,32,128]{2,1,0:T(8,128)S(1)} fusion(bf16[512,4,32]{0,2,1:T(8,128)(2,1)} %bitcast.83, f32[4,128]{1,0:T(4,128)S(1)} %fusion.71, f32[4,128,512]{2,1,0:T(8,128)S(1)} %fusion.37), kind=kOutput, calls=%fused_computation.64 | convolution fusion | flops 17564672 | bytes 1247232 | tf_op jit(solution)/shard_map/hrl,lhd->rhd/dot_general | solution.py:59
  41.9 31.5 %all_gather.11 = bf16[128,1024]{0,1:T(8,128)(2,1)S(1)} all-gather(bf16[128,128]{0,1:T(8,128)(2,1)S(1)} %fusion.66), channel_id=1, replica_groups=mesh['rows'=4,'cols'=8] {'cols'}, dimensions={1}, use_global_device_ids=true | all-gather | bytes 294912 | tf_op jit(solution)/shard_map/all_gather | solution.py:62
  74.7 10.3 %psum.7 = bf16[64,64]{0,1:T(8,128)(2,1)S(1)} all-reduce(bf16[64,64]{0,1:T(8,128)(2,1)S(1)} %dynamic-slice_select_fusion), channel_id=1, replica_groups=mesh['rows'=4,'cols'=8] {'rows'}, use_global_device_ids=true, to_apply=%region_8.9 | all-reduce | flops 4096 | bytes 16384 | tf_op jit(solution)/shard_map/psum | solution.py:12
  85.2 15.0 %while.10 = (s32[]{:T(128)}, bf16[2,64,64,128]{3,2,1,0:T(8,128)(2,1)}, bf16[2,64,64,128]{3,2,1,0:T(8,128)(2,1)}, bf16[2,64,64]{2,1,0:T(8,128)(2,1)S(1)}, bf16[64...) while((s32[]{:T(128)}, ...), condition=%wide.region_12.13_spmd, body=%wide.region_9.12_spmd.sunk | while | flops 1223700480 | bytes 17334912 | solution.py:97
  85.8 1.0 copy-done.2
  86.8 1.2 %convert_reduce_fusion.5 = (f32[64,64]{1,0:T(8,128)S(1)}, bf16[64,64,128]{2,1,0:T(8,128)(2,1)S(1)}) fusion(bf16[128,128]{1,0:T(8,128)(2,1)S(1)} %get-tuple-element.184, bf16[64,64,64]{2,1,0:T(8,128)(2,1)S(1)} %get-tuple-element.157, bf16[64,64,64]{2,1,0:T(8,128)(2,1)S(1)} %get-tuple-element.158, bf16[2,64,64,128]{3,2,1,0:T(8,128)(2,1)S(1)} %copy-done.2, ...), kind=kOutput, calls=%fused_computation.6.clone.1 | convolution fusion | flops 138932224 | bytes 3194884 | tf_op jit(solution)/shard_map/while/body/eval_jaxpr/rcq,qp->rcp/dot_general | solution.py:86
  88.1 1.3 %fusion.89 = f32[64,64]{1,0:T(8,128)S(1)} fusion(bf16[64,64,128]{2,1,0:T(8,128)(2,1)S(1)} %get-tuple-element.159, f32[64,64]{1,0:T(8,128)S(1)} %broadcast_multiply_fusion.5), kind=kLoop, calls=%fused_computation.9.clone.1 | loop fusion | flops 2093056 | bytes 1081344 | tf_op jit(solution)/shard_map/while/body/eval_jaxpr/reduce_sum | solution.py:18
  89.4 3.4 %fusion.90 = bf16[2,64,64,128]{3,2,1,0:T(8,128)(2,1)} fusion(bf16[2,64,64,128]{3,2,1,0:T(8,128)(2,1)} %get-tuple-element.171, s32[]{:T(128)} %get-tuple-element.170, bf16[64,64,128]{2,1,0:T(8,128)(2,1)S(1)} %get-tuple-element.159, f32[64,64]{1,0:T(8,128)S(1)} %add_rsqrt_fusion.5, f32[64,64]{1,0:T(8,128)S(1)} %broadcast_multiply_fusion.5, ...), kind=kOutput, calls=%fused_computation.17.clone.1 | convolution fusion | flops 1081606144 | bytes 3473920 | tf_op jit(solution)/shard_map/while/body/eval_jaxpr/rck,kp->rcp/dot_general | solution.py:94
  93.3 1.0 %copy-done.2 = bf16[2,64,64,128]{3,2,1,0:T(8,128)(2,1)S(1)} copy-done((bf16[2,64,64,128]{3,2,1,0:T(8,128)(2,1)S(1)}, bf16[2,64,64,128]{3,2,1,0:T(8,128)(2,1)}, u32[]{:S(2)}) %copy-start.2) | copy-done | bytes 2097176 | tf_op jit(solution)/shard_map/while
  94.4 1.2 %convert_reduce_fusion.5 = (f32[64,64]{1,0:T(8,128)S(1)}, bf16[64,64,128]{2,1,0:T(8,128)(2,1)S(1)}) fusion(bf16[128,128]{1,0:T(8,128)(2,1)S(1)} %get-tuple-element.184, bf16[64,64,64]{2,1,0:T(8,128)(2,1)S(1)} %get-tuple-element.157, bf16[64,64,64]{2,1,0:T(8,128)(2,1)S(1)} %get-tuple-element.158, bf16[2,64,64,128]{3,2,1,0:T(8,128)(2,1)S(1)} %copy-done.2, ...), kind=kOutput, calls=%fused_computation.6.clone.1 | convolution fusion | flops 138932224 | bytes 3194884 | tf_op jit(solution)/shard_map/while/body/eval_jaxpr/rcq,qp->rcp/dot_general | solution.py:86
  95.6 1.3 %fusion.89 = f32[64,64]{1,0:T(8,128)S(1)} fusion(bf16[64,64,128]{2,1,0:T(8,128)(2,1)S(1)} %get-tuple-element.159, f32[64,64]{1,0:T(8,128)S(1)} %broadcast_multiply_fusion.5), kind=kLoop, calls=%fused_computation.9.clone.1 | loop fusion | flops 2093056 | bytes 1081344 | tf_op jit(solution)/shard_map/while/body/eval_jaxpr/reduce_sum | solution.py:18
  96.9 3.4 %fusion.90 = bf16[2,64,64,128]{3,2,1,0:T(8,128)(2,1)} fusion(bf16[2,64,64,128]{3,2,1,0:T(8,128)(2,1)} %get-tuple-element.171, s32[]{:T(128)} %get-tuple-element.170, bf16[64,64,128]{2,1,0:T(8,128)(2,1)S(1)} %get-tuple-element.159, f32[64,64]{1,0:T(8,128)S(1)} %add_rsqrt_fusion.5, f32[64,64]{1,0:T(8,128)S(1)} %broadcast_multiply_fusion.5, ...), kind=kOutput, calls=%fused_computation.17.clone.1 | convolution fusion | flops 1081606144 | bytes 3473920 | tf_op jit(solution)/shard_map/while/body/eval_jaxpr/rck,kp->rcp/dot_general | solution.py:94
  (58 shorter events, 6.2 us)
Async XLA Ops:
  0.6 72.8 %copy-start = (bf16[1024,1024]{1,0:T(8,128)(2,1)S(1)}, bf16[1024,1024]{1,0:T(8,128)(2,1)}, u32[]{:S(2)}) copy-start(bf16[1024,1024]{1,0:T(8,128)(2,1)} %param.17) | copy-start | bytes 6291460
  0.6 2.9 %copy-start.1 = (bf16[128,64,128]{2,1,0:T(8,128)(2,1)S(1)}, bf16[128,64,128]{2,1,0:T(8,128)(2,1)}, u32[]{:S(2)}) copy-start(bf16[128,64,128]{2,1,0:T(8,128)(2,1)} %param.13) | copy-start | bytes 6291460
  6.4 3.4 %copy-start.7 = (bf16[128,32]{0,1:T(8,128)(2,1)S(1)}, bf16[128,32]{0,1:T(8,128)(2,1)}, u32[]{:S(2)}) copy-start(bf16[128,32]{0,1:T(8,128)(2,1)} %param.15) | copy-start | bytes 24580
  9.7 9.7 %copy-start.3 = (bf16[128,1024]{1,0:T(8,128)(2,1)S(1)}, bf16[128,1024]{1,0:T(8,128)(2,1)}, u32[]{:S(2)}) copy-start(bf16[128,1024]{1,0:T(8,128)(2,1)} %param.12) | copy-start | bytes 786436
  12.2 22.4 %all-to-all-start = ((bf16[32,128,64]{1,2,0:T(8,128)(2,1)}), bf16[32,128,64]{1,2,0:T(8,128)(2,1)}, u32[]{:S(2)}, u32[]{:S(2)}) async-start(bf16[32,128,64]{1,2,0:T(8,128)(2,1)} %copy.31), calls=%async_computation | async-start | bytes 1048576 | tf_op jit(solution)/shard_map/all_to_all | solution.py:41
  19.8 14.7 %copy-start.8 = (s32[512]{0:T(512)S(1)}, s32[512]{0:T(512)}, u32[]{:S(2)}) copy-start(s32[512]{0:T(512)} %param.14) | copy-start | bytes 6148
  21.9 0.7 copy-start.4
  41.0 33.3 %copy-start.9 = (bf16[1024,128]{1,0:T(8,128)(2,1)S(1)}, bf16[1024,128]{1,0:T(8,128)(2,1)}, u32[]{:S(2)}) copy-start(bf16[1024,128]{1,0:T(8,128)(2,1)} %param.18) | copy-start | bytes 786436
  41.9 43.3 %copy-start.6 = (bf16[128,128]{1,0:T(8,128)(2,1)S(1)}, bf16[128,128]{1,0:T(8,128)(2,1)}, u32[]{:S(2)}) copy-start(bf16[128,128]{1,0:T(8,128)(2,1)} %param.19) | copy-start | bytes 98308
  41.9 43.3 %copy-start.10 = (bf16[128,512]{1,0:T(8,128)(2,1)S(1)}, bf16[128,512]{1,0:T(8,128)(2,1)}, u32[]{:S(2)}) copy-start(bf16[128,512]{1,0:T(8,128)(2,1)} %param.20) | copy-start | bytes 393220
  41.9 43.3 %copy-start.11 = (bf16[512,128]{1,0:T(8,128)(2,1)S(1)}, bf16[512,128]{1,0:T(8,128)(2,1)}, u32[]{:S(2)}) copy-start(bf16[512,128]{1,0:T(8,128)(2,1)} %param.21) | copy-start | bytes 393220
  74.0 11.2 %copy-start.5 = (bf16[128,1024]{1,0:T(8,128)(2,1)}, bf16[128,1024]{1,0:T(8,128)(2,1)S(1)}, u32[]{:S(2)}) copy-start(bf16[128,1024]{1,0:T(8,128)(2,1)S(1)} %get-tuple-element.103) | copy-start | bytes 786436
  85.2 1.6 %copy-start.2 = (bf16[2,64,64,128]{3,2,1,0:T(8,128)(2,1)S(1)}, bf16[2,64,64,128]{3,2,1,0:T(8,128)(2,1)}, u32[]{:S(2)}) copy-start(bf16[2,64,64,128]{3,2,1,0:T(8,128)(2,1)} %get-tuple-element.181) | copy-start | bytes 6291460 | tf_op jit(solution)/shard_map/while
  92.8 1.6 %copy-start.2 = (bf16[2,64,64,128]{3,2,1,0:T(8,128)(2,1)S(1)}, bf16[2,64,64,128]{3,2,1,0:T(8,128)(2,1)}, u32[]{:S(2)}) copy-start(bf16[2,64,64,128]{3,2,1,0:T(8,128)(2,1)} %get-tuple-element.181) | copy-start | bytes 6291460 | tf_op jit(solution)/shard_map/while
where the time goes:
time: 101 us; the launch traced here: 100 us
  blocking collectives  53.1 us (53%)
  other arithmetic  15.9 us (16%)
  matrix products  15.5 us (15%)
  local copies, waits for them, and re-layouts  7.51 us (7%)
  starting transfers between devices  7.28 us (7%)
    all_gather x1, blocking collectives, per_device(): whole_heads = lax.all_gather(mixed, 'cols', axis=1, tiled=True)  31.5 us
    psum x1, blocking collectives, from_root(): return lax.psum(jnp.where(mine, value, jnp.zeros_like(value)), axis)  10.3 us
    all_to_all x1, starting transfers between devices, per_device(): lax.all_to_all(bias_local, 'cols', split_axis=0, concat_axis=2, tiled=True)  7.28 us
    dot_general x2, matrix products, update_block(): jnp.einsum('rck,kp->rcp', hidden, w_down, preferred_element_type=jnp.floa...  6.75 us
    all_gather x1, blocking collectives, per_device(): lax.all_gather(value_local, 'rows', axis=0, tiled=True)  5.88 us
    reduce_sum x5, other arithmetic, layer_norm(): jnp.mean(centred * centred, -1, keepdims=True) + epsilon  5.77 us
    all_gather x1, blocking collectives, per_device(): lax.all_gather(key_local, 'rows', axis=0, tiled=True)  5.43 us
    convert_element_type x1, other arithmetic, per_device(): normed_pair = layer_norm(pair).astype(jnp.bfloat16)  3.36 us
  transfers between devices with their start and end apart: 1, of which 0 were waited for; matrix products, arithmetic and copies ran while one was open for 3% of the time, Pallas kernels for 0%

commit v1 on v0

--- a/solution.py
+++ b/solution.py
@@ -3,13 +3,15 @@
 import jax.numpy as jnp
 from jax import lax
 from jax.sharding import PartitionSpec as P
+from jax.lax import all_gather
 
 epsilon = 1e-05
 
 
 def from_root(value, axis, root):
     mine = lax.axis_index(axis) == root
-    return lax.psum(jnp.where(mine, value, jnp.zeros_like(value)), axis)
+    vector_pass = lambda point, axis_id: jnp.sum(all_gather(point, axis_id), axis=0)
+    return vector_pass(jnp.where(mine, value, jnp.zeros_like(value)), axis)
 
 
 def layer_norm(values):

time: 101 us -> 95.7 us (0.948)
  blocking collectives: 53.1 us -> 48.1 us
    psum x1 -> x0, blocking collectives: 10.3 us -> none  [from_root(): return lax.psum(jnp.where(mine, value, jnp.zeros_like(value)), axis)]
    all_gather x0 -> x1, blocking collectives: none -> 5.42 us  [from_root(): all_gather(point, axis_id)]
where the time goes in v1:
time: 95.7 us; the launch traced here: 95.3 us
  blocking collectives  48.1 us (50%)
  other arithmetic  15.9 us (17%)
  matrix products  15.5 us (16%)
  local copies, waits for them, and re-layouts  7.5 us (8%)
  starting transfers between devices  7.28 us (8%)
    all_gather x1, blocking collectives, per_device(): whole_heads = lax.all_gather(mixed, 'cols', axis=1, tiled=True)  31.4 us
    all_to_all x1, starting transfers between devices, per_device(): lax.all_to_all(bias_local, 'cols', split_axis=0, concat_axis=2, tiled=True)  7.28 us
    dot_general x2, matrix products, update_block(): jnp.einsum('rck,kp->rcp', hidden, w_down, preferred_element_type=jnp.floa...  6.76 us
    all_gather x1, blocking collectives, per_device(): lax.all_gather(value_local, 'rows', axis=0, tiled=True)  5.88 us
    reduce_sum x5, other arithmetic, layer_norm(): jnp.mean(centred * centred, -1, keepdims=True) + epsilon  5.77 us
    all_gather x1, blocking collectives, per_device(): lax.all_gather(key_local, 'rows', axis=0, tiled=True)  5.43 us
    all_gather x1, blocking collectives, from_root(): all_gather(point, axis_id)  5.42 us
    convert_element_type x1, other arithmetic, per_device(): normed_pair = layer_norm(pair).astype(jnp.bfloat16)  3.36 us
  transfers between devices with their start and end apart: 1, of which 0 were waited for; matrix products, arithmetic and copies ran while one was open for 3% of the time, Pallas kernels for 0%

profile of v1, /device:TPU:0, one launch (start us, length us, event | category | flops | bytes accessed | tf_op | source)
XLA Modules:
  0.0 95.3 jit_solution(412793346455693006)
XLA Ops:
  0.7 2.9 %convert_reduce_fusion.1 = f32[128,64]{1,0:T(8,128)S(1)} fusion(bf16[128,64,128]{2,1,0:T(8,128)(2,1)} %param.13), kind=kLoop, calls=%fused_computation.33 | loop fusion | flops 2088960 | bytes 2129920 | tf_op jit(solution)/shard_map/reduce_sum | solution.py:19
  3.6 2.7 %fusion.30 = f32[128,64]{1,0:T(8,128)S(1)} fusion(bf16[128,64,128]{2,1,0:T(8,128)(2,1)S(1)} %copy-done.1, f32[128,64]{1,0:T(8,128)S(1)} %broadcast_multiply_fusion.1), kind=kLoop, calls=%fused_computation.36 | loop fusion | flops 4186112 | bytes 2162688 | tf_op jit(solution)/shard_map/reduce_sum | solution.py:20
  6.4 3.4 %fusion.31 = bf16[128,64,128]{2,1,0:T(8,128)(2,1)S(1)} fusion(bf16[128,64,128]{2,1,0:T(8,128)(2,1)S(1)} %copy-done.1, f32[128,64]{1,0:T(8,128)S(1)} %add_rsqrt_fusion.1, f32[128,64]{1,0:T(8,128)S(1)} %broadcast_multiply_fusion.1), kind=kLoop, calls=%fused_computation.37 | loop fusion | flops 4194304 | bytes 4259840 | tf_op jit(solution)/shard_map/convert_element_type | solution.py:28
  9.8 1.4 %fusion.41 = bf16[32,128,64]{1,0,2:T(8,128)(2,1)S(1)} fusion(bf16[128,64,128]{2,1,0:T(8,128)(2,1)S(1)} %fusion.31, bf16[128,32]{0,1:T(8,128)(2,1)S(1)} %copy-done.7), kind=kOutput, calls=%fused_computation.46 | convolution fusion | flops 67371008 | bytes 2629632 | tf_op jit(solution)/shard_map/rcp,ph->hrc/dot_general | solution.py:29
  11.1 1.0 %copy.31 = bf16[32,128,64]{1,2,0:T(8,128)(2,1)} copy(bf16[32,128,64]{1,0,2:T(8,128)(2,1)S(1)} %fusion.41) | data formatting | bytes 1048576 | tf_op jit(solution)/shard_map/convert_element_type | solution.py:31
  12.2 7.3 %all-to-all-start = ((bf16[32,128,64]{1,2,0:T(8,128)(2,1)}), bf16[32,128,64]{1,2,0:T(8,128)(2,1)}, u32[]{:S(2)}, u32[]{:S(2)}) async-start(bf16[32,128,64]{1,2,0:T(8,128)(2,1)} %copy.31), calls=%async_computation | async-start | bytes 1048576 | tf_op jit(solution)/shard_map/all_to_all | solution.py:43
  19.9 1.5 %copy.29 = bf16[4,1024,128]{1,2,0:T(8,128)(2,1)S(1)} copy(bf16[4,1024,128]{2,1,0:T(8,128)(2,1)} %param.16) | data formatting | bytes 2097152 | tf_op args[4]
  23.2 5.4 %all-gather.1 = bf16[1,512,128]{1,2,0:T(8,128)(2,1)S(1)} all-gather(bf16[1,128,128]{1,2,0:T(8,128)(2,1)S(1)} %get-tuple-element.97), channel_id=3, replica_groups=mesh['rows'=4,'cols'=8] {'rows'}, dimensions={1}, use_global_device_ids=true | all-gather | bytes 163840 | tf_op jit(solution)/shard_map/all_gather | solution.py:45
  28.7 5.9 %all-gather = bf16[1,512,128]{1,2,0:T(8,128)(2,1)} all-gather(bf16[1,128,128]{1,2,0:T(8,128)(2,1)S(1)} %get-tuple-element.99), channel_id=2, replica_groups=mesh['rows'=4,'cols'=8] {'rows'}, dimensions={1}, use_global_device_ids=true | all-gather | bytes 163840 | tf_op jit(solution)/shard_map/all_gather | solution.py:46
  34.5 1.1 %convert_bitcast_fusion = f32[4,128,8,64]{1,3,0,2:T(8,128)S(1)} fusion(bf16[8,4,128,64]{2,3,1,0:T(8,128)(2,1)} %bitcast.29), kind=kLoop, calls=%fused_computation.50 | loop fusion | flops 262144 | bytes 1572864 | tf_op jit(solution)/shard_map/convert_element_type | solution.py:57
  35.8 1.3 %copy.33 = f32[4,128,512]{2,1,0:T(8,128)} copy(f32[4,128,512]{1,2,0:T(8,128)S(1)} %bitcast.78) | data formatting | bytes 2097152 | tf_op jit(solution)/shard_map/convert_element_type | solution.py:57
  37.1 1.6 %fusion.37 = f32[4,128,512]{2,1,0:T(8,128)S(1)} fusion(f32[4,128,512]{2,1,0:T(8,128)} %copy.33, bf16[128,4,32]{0,2,1:T(8,128)(2,1)} %bitcast.84, bf16[512,4,32]{0,2,1:T(8,128)(2,1)S(1)} %bitcast.81, pred[512]{0:T(512)(128)(4,1)S(1)} %broadcast_compare_fusion), kind=kOutput, calls=%fused_computation.44 | convolution fusion | flops 17563648 | bytes 2261504 | tf_op jit(solution)/shard_map/rhd,lhd->hrl/dot_general | solution.py:55
  39.0 1.9 %fusion.53 = f32[4,32,128]{2,1,0:T(8,128)S(1)} fusion(bf16[512,4,32]{0,2,1:T(8,128)(2,1)} %bitcast.85, f32[4,128]{1,0:T(4,128)S(1)} %fusion.71, f32[4,128,512]{2,1,0:T(8,128)S(1)} %fusion.37), kind=kOutput, calls=%fused_computation.64 | convolution fusion | flops 17564672 | bytes 1247232 | tf_op jit(solution)/shard_map/hrl,lhd->rhd/dot_general | solution.py:61
  41.9 31.4 %all_gather.17 = bf16[128,1024]{0,1:T(8,128)(2,1)S(1)} all-gather(bf16[128,128]{0,1:T(8,128)(2,1)S(1)} %fusion.66), channel_id=1, replica_groups=mesh['rows'=4,'cols'=8] {'cols'}, dimensions={1}, use_global_device_ids=true | all-gather | bytes 294912 | tf_op jit(solution)/shard_map/all_gather | solution.py:64
  74.6 5.4 %all-gather.2 = bf16[256,64]{1,0:T(8,128)(2,1)S(1)} all-gather(bf16[64,64]{1,0:T(8,128)(2,1)S(1)} %copy.34), channel_id=4, replica_groups=mesh['rows'=4,'cols'=8] {'rows'}, dimensions={0}, use_global_device_ids=true | all-gather | bytes 40960 | tf_op jit(solution)/shard_map/all_gather | solution.py:13
  80.2 15.1 %while.10 = (s32[]{:T(128)}, bf16[2,64,64,128]{3,2,1,0:T(8,128)(2,1)}, bf16[2,64,64,128]{3,2,1,0:T(8,128)(2,1)}, bf16[2,64,64]{2,1,0:T(8,128)(2,1)S(1)}, bf16[64...) while((s32[]{:T(128)}, ...), condition=%wide.region_12.13_spmd, body=%wide.region_9.12_spmd.sunk | while | flops 1223700480 | bytes 17334912 | solution.py:99
  80.8 1.0 %copy-done.2 = bf16[2,64,64,128]{3,2,1,0:T(8,128)(2,1)S(1)} copy-done((bf16[2,64,64,128]{3,2,1,0:T(8,128)(2,1)S(1)}, bf16[2,64,64,128]{3,2,1,0:T(8,128)(2,1)}, u32[]{:S(2)}) %copy-start.2) | copy-done | bytes 2097176 | tf_op jit(solution)/shard_map/while
  81.8 1.2 %convert_reduce_fusion.5 = (f32[64,64]{1,0:T(8,128)S(1)}, bf16[64,64,128]{2,1,0:T(8,128)(2,1)S(1)}) fusion(bf16[128,128]{1,0:T(8,128)(2,1)S(1)} %get-tuple-element.184, bf16[64,64,64]{2,1,0:T(8,128)(2,1)S(1)} %get-tuple-element.157, bf16[64,64,64]{2,1,0:T(8,128)(2,1)S(1)} %get-tuple-element.158, bf16[2,64,64,128]{3,2,1,0:T(8,128)(2,1)S(1)} %copy-done.2, ...), kind=kOutput, calls=%fused_computation.6.clone.1 | convolution fusion | flops 138932224 | bytes 3194884 | tf_op jit(solution)/shard_map/while/body/eval_jaxpr/rcq,qp->rcp/dot_general | solution.py:88
  83.1 1.3 %fusion.89 = f32[64,64]{1,0:T(8,128)S(1)} fusion(bf16[64,64,128]{2,1,0:T(8,128)(2,1)S(1)} %get-tuple-element.159, f32[64,64]{1,0:T(8,128)S(1)} %broadcast_multiply_fusion.5), kind=kLoop, calls=%fused_computation.9.clone.1 | loop fusion | flops 2093056 | bytes 1081344 | tf_op jit(solution)/shard_map/while/body/eval_jaxpr/reduce_sum | solution.py:20
  84.4 3.4 %fusion.90 = bf16[2,64,64,128]{3,2,1,0:T(8,128)(2,1)} fusion(bf16[2,64,64,128]{3,2,1,0:T(8,128)(2,1)} %get-tuple-element.171, s32[]{:T(128)} %get-tuple-element.170, bf16[64,64,128]{2,1,0:T(8,128)(2,1)S(1)} %get-tuple-element.159, f32[64,64]{1,0:T(8,128)S(1)} %add_rsqrt_fusion.5, f32[64,64]{1,0:T(8,128)S(1)} %broadcast_multiply_fusion.5, ...), kind=kOutput, calls=%fused_computation.17.clone.1 | convolution fusion | flops 1081606144 | bytes 3473920 | tf_op jit(solution)/shard_map/while/body/eval_jaxpr/rck,kp->rcp/dot_general | solution.py:96
  88.3 1.0 %copy-done.2 = bf16[2,64,64,128]{3,2,1,0:T(8,128)(2,1)S(1)} copy-done((bf16[2,64,64,128]{3,2,1,0:T(8,128)(2,1)S(1)}, bf16[2,64,64,128]{3,2,1,0:T(8,128)(2,1)}, u32[]{:S(2)}) %copy-start.2) | copy-done | bytes 2097176 | tf_op jit(solution)/shard_map/while
  89.4 1.2 %convert_reduce_fusion.5 = (f32[64,64]{1,0:T(8,128)S(1)}, bf16[64,64,128]{2,1,0:T(8,128)(2,1)S(1)}) fusion(bf16[128,128]{1,0:T(8,128)(2,1)S(1)} %get-tuple-element.184, bf16[64,64,64]{2,1,0:T(8,128)(2,1)S(1)} %get-tuple-element.157, bf16[64,64,64]{2,1,0:T(8,128)(2,1)S(1)} %get-tuple-element.158, bf16[2,64,64,128]{3,2,1,0:T(8,128)(2,1)S(1)} %copy-done.2, ...), kind=kOutput, calls=%fused_computation.6.clone.1 | convolution fusion | flops 138932224 | bytes 3194884 | tf_op jit(solution)/shard_map/while/body/eval_jaxpr/rcq,qp->rcp/dot_general | solution.py:88
  90.6 1.3 %fusion.89 = f32[64,64]{1,0:T(8,128)S(1)} fusion(bf16[64,64,128]{2,1,0:T(8,128)(2,1)S(1)} %get-tuple-element.159, f32[64,64]{1,0:T(8,128)S(1)} %broadcast_multiply_fusion.5), kind=kLoop, calls=%fused_computation.9.clone.1 | loop fusion | flops 2093056 | bytes 1081344 | tf_op jit(solution)/shard_map/while/body/eval_jaxpr/reduce_sum | solution.py:20
  91.9 3.4 %fusion.90 = bf16[2,64,64,128]{3,2,1,0:T(8,128)(2,1)} fusion(bf16[2,64,64,128]{3,2,1,0:T(8,128)(2,1)} %get-tuple-element.171, s32[]{:T(128)} %get-tuple-element.170, bf16[64,64,128]{2,1,0:T(8,128)(2,1)S(1)} %get-tuple-element.159, f32[64,64]{1,0:T(8,128)S(1)} %add_rsqrt_fusion.5, f32[64,64]{1,0:T(8,128)S(1)} %broadcast_multiply_fusion.5, ...), kind=kOutput, calls=%fused_computation.17.clone.1 | convolution fusion | flops 1081606144 | bytes 3473920 | tf_op jit(solution)/shard_map/while/body/eval_jaxpr/rck,kp->rcp/dot_general | solution.py:96
  (59 shorter events, 6.2 us)
Async XLA Ops:
  0.6 72.6 %copy-start = (bf16[1024,1024]{1,0:T(8,128)(2,1)S(1)}, bf16[1024,1024]{1,0:T(8,128)(2,1)}, u32[]{:S(2)}) copy-start(bf16[1024,1024]{1,0:T(8,128)(2,1)} %param.17) | copy-start | bytes 6291460
  0.6 2.9 %copy-start.1 = (bf16[128,64,128]{2,1,0:T(8,128)(2,1)S(1)}, bf16[128,64,128]{2,1,0:T(8,128)(2,1)}, u32[]{:S(2)}) copy-start(bf16[128,64,128]{2,1,0:T(8,128)(2,1)} %param.13) | copy-start | bytes 6291460
  6.4 3.4 %copy-start.7 = (bf16[128,32]{0,1:T(8,128)(2,1)S(1)}, bf16[128,32]{0,1:T(8,128)(2,1)}, u32[]{:S(2)}) copy-start(bf16[128,32]{0,1:T(8,128)(2,1)} %param.15) | copy-start | bytes 24580
  9.7 9.7 %copy-start.3 = (bf16[128,1024]{1,0:T(8,128)(2,1)S(1)}, bf16[128,1024]{1,0:T(8,128)(2,1)}, u32[]{:S(2)}) copy-start(bf16[128,1024]{1,0:T(8,128)(2,1)} %param.12) | copy-start | bytes 786436
  12.2 22.4 %all-to-all-start = ((bf16[32,128,64]{1,2,0:T(8,128)(2,1)}), bf16[32,128,64]{1,2,0:T(8,128)(2,1)}, u32[]{:S(2)}, u32[]{:S(2)}) async-start(bf16[32,128,64]{1,2,0:T(8,128)(2,1)} %copy.31), calls=%async_computation | async-start | bytes 1048576 | tf_op jit(solution)/shard_map/all_to_all | solution.py:43
  19.8 14.7 %copy-start.8 = (s32[512]{0:T(512)S(1)}, s32[512]{0:T(512)}, u32[]{:S(2)}) copy-start(s32[512]{0:T(512)} %param.14) | copy-start | bytes 6148
  21.9 0.7 copy-start.4
  41.0 33.1 %copy-start.9 = (bf16[1024,128]{1,0:T(8,128)(2,1)S(1)}, bf16[1024,128]{1,0:T(8,128)(2,1)}, u32[]{:S(2)}) copy-start(bf16[1024,128]{1,0:T(8,128)(2,1)} %param.18) | copy-start | bytes 786436
  73.3 6.9 %copy-start.6 = (bf16[128,128]{1,0:T(8,128)(2,1)S(1)}, bf16[128,128]{1,0:T(8,128)(2,1)}, u32[]{:S(2)}) copy-start(bf16[128,128]{1,0:T(8,128)(2,1)} %param.19) | copy-start | bytes 98308
  73.3 6.9 %copy-start.10 = (bf16[128,512]{1,0:T(8,128)(2,1)S(1)}, bf16[128,512]{1,0:T(8,128)(2,1)}, u32[]{:S(2)}) copy-start(bf16[128,512]{1,0:T(8,128)(2,1)} %param.20) | copy-start | bytes 393220
  73.3 6.9 %copy-start.11 = (bf16[512,128]{1,0:T(8,128)(2,1)S(1)}, bf16[512,128]{1,0:T(8,128)(2,1)}, u32[]{:S(2)}) copy-start(bf16[512,128]{1,0:T(8,128)(2,1)} %param.21) | copy-start | bytes 393220
  73.8 6.4 %copy-start.5 = (bf16[128,1024]{1,0:T(8,128)(2,1)}, bf16[128,1024]{1,0:T(8,128)(2,1)S(1)}, u32[]{:S(2)}) copy-start(bf16[128,1024]{1,0:T(8,128)(2,1)S(1)} %get-tuple-element.103) | copy-start | bytes 786436
  80.2 1.6 %copy-start.2 = (bf16[2,64,64,128]{3,2,1,0:T(8,128)(2,1)S(1)}, bf16[2,64,64,128]{3,2,1,0:T(8,128)(2,1)}, u32[]{:S(2)}) copy-start(bf16[2,64,64,128]{3,2,1,0:T(8,128)(2,1)} %get-tuple-element.181) | copy-start | bytes 6291460 | tf_op jit(solution)/shard_map/while
  87.8 1.6 %copy-start.2 = (bf16[2,64,64,128]{3,2,1,0:T(8,128)(2,1)S(1)}, bf16[2,64,64,128]{3,2,1,0:T(8,128)(2,1)}, u32[]{:S(2)}) copy-start(bf16[2,64,64,128]{3,2,1,0:T(8,128)(2,1)} %get-tuple-element.181) | copy-start | bytes 6291460 | tf_op jit(solution)/shard_map/while
